TPU v7x, 1024 devices: a whole 4x8x16 slice. The times are simulated.
1024 devices in a mesh: dp: 16 (over z), tensor: 8 (over y_lo, core), section: 8 (over x, y_hi).
Axes of the slice: x: 4, y: 8 (y_hi: 2, y_lo: 4; y = y_hi * 4 + y_lo), z: 16, core: 2. Of those that a mesh axis runs over, the one named last changes fastest.
Arguments:
- tokens: bfloat16 [1024, 8192], P('section', 'tensor'), may hold values from -6 to 6
- cotangent: bfloat16 [1024, 8192], P('section', 'tensor'), may hold values from -6 to 6
- gate_weight: bfloat16 [8192, 15360], P(('tensor', 'section'), 'dp'), may hold values from -0.0625 to 0.0625
- up_weight: bfloat16 [8192, 15360], P(('tensor', 'section'), 'dp'), may hold values from -0.0625 to 0.0625
- down_weight: bfloat16 [8192, 15360], P(('tensor', 'section'), 'dp'), may hold values from -0.046875 to 0.046875
Outputs:
- mixed: bfloat16 [1024, 8192], P(('section', 'dp'), 'tensor')
- input_grad: bfloat16 [1024, 8192], P(('section', 'dp'), 'tensor')
All inputs are finite; a program needn't handle non-finite values.
Results may differ from a plain program's by a relative error of at most 0.005.
Values may be sent and summed in bfloat16 or wider, within the bound.
A program may use at most 64 MiB of HBM per device.

v0:
```python
import jax
import jax.numpy as jnp
from jax import lax
from jax.sharding import PartitionSpec as P


def in_one_piece(arrays, axis, dim, along):
    ends, at = ([], 0)
    for a in arrays[:-1]:
        at += a.shape[along]
        ends.append(at)
    both = jnp.concatenate(arrays, axis=along)
    return tuple(jnp.split(lax.all_gather(both, axis, axis=dim, tiled=True), ends, axis=along))


def cut_along(array, dim, length):
    shape = array.shape
    parts = array.reshape(*shape[:dim], length, shape[dim] // length, *shape[dim + 1 :])
    return jnp.moveaxis(parts, dim, 0)


def sent_and_summed(array, axis, dim):
    parts = cut_along(array, dim, lax.axis_size(axis))
    arrived = lax.all_to_all(parts, axis, split_axis=0, concat_axis=0, tiled=True)
    return arrived.sum(axis=0)


def sent_together(arrays, axis, dim, along):
    both = jnp.concatenate(arrays, axis=along)
    filled, at, done = (sent_and_summed(both, axis, dim), 0, [])
    for a in arrays:
        done.append(lax.slice_in_dim(filled, at, at + a.shape[along], axis=along))
        at += a.shape[along]
    return tuple(done)


def for_sending(array):

    def short(part):
        return part.astype(jnp.bfloat16) if part.dtype == jnp.float32 else part

    return jax.tree.map(short, array)


def in_order(parts, dim):
    parts = jnp.moveaxis(parts, 0, dim)
    shape = parts.shape
    return parts.reshape(*shape[:dim], shape[dim] * shape[dim + 1], *shape[dim + 2 :])


def from_everyone(array, axis):
    copies = jnp.broadcast_to(array, (lax.axis_size(axis), *array.shape))
    return lax.all_to_all(copies, axis, split_axis=0, concat_axis=0, tiled=True)


def gathered_copies(array, axis, dim):
    return in_order(from_everyone(array, axis), dim)


def activate(gate, up):
    sig = jax.nn.sigmoid(gate)
    return (gate * sig * up).astype(jnp.bfloat16)


def gradients(back, gate, up):
    sig = jax.nn.sigmoid(gate)
    gate_grad = (back * up * sig * (1.0 + gate * (1.0 - sig))).astype(jnp.bfloat16)
    up_grad = (back * gate * sig).astype(jnp.bfloat16)
    return (gate_grad, up_grad)


def body(tokens, cotangent, gate_weight, up_weight, down_weight):
    gate_new, up_new, down_new = in_one_piece(
        (gate_weight, up_weight, down_weight), "section", 0, 1
    )
    contract = (((1,), (1,)), ((), ()))
    gate_part = jnp.dot(tokens, gate_new, preferred_element_type=jnp.float32)
    up_part = jnp.dot(tokens, up_new, preferred_element_type=jnp.float32)
    gate, up = sent_together((gate_part, up_part), "tensor", 0, 1)
    hidden = lax.all_gather(activate(gate, up), "tensor", axis=0, tiled=True)
    output_part = lax.dot_general(hidden, down_new, contract, preferred_element_type=jnp.float32)
    back_part = jnp.dot(cotangent, down_new, preferred_element_type=jnp.float32)
    back = sent_and_summed(back_part, "tensor", 0)
    gate_grad, up_grad = jax.tree.map(
        lambda part: gathered_copies(part, "tensor", 0), for_sending(gradients(back, gate, up))
    )
    grad_part = lax.dot_general(gate_grad, gate_new, contract, preferred_element_type=jnp.float32)
    grad_part = grad_part + lax.dot_general(
        up_grad, up_new, contract, preferred_element_type=jnp.float32
    )
    mixed, input_grad = sent_together((output_part, grad_part), "dp", 0, 1)
    return (mixed.astype(jnp.bfloat16), input_grad.astype(jnp.bfloat16))


def solution(mesh):
    placed = (
        P("section", "tensor"),
        P("section", "tensor"),
        P(("tensor", "section"), "dp"),
        P(("tensor", "section"), "dp"),
        P(("tensor", "section"), "dp"),
    )
    return jax.shard_map(
        body,
        mesh=mesh,
        in_specs=placed,
        out_specs=(P(("section", "dp"), "tensor"), P(("section", "dp"), "tensor")),
        check_vma=False,
    )
```

profile of v0, /device:TPU:1, one launch (start us, length us, event | category | flops | bytes accessed | tf_op | source)
XLA Modules:
  0.0 329.1 jit_solution(9515775680443432031)
XLA Ops:
  7.2 0.0 copy-start
  7.2 0.0 copy-start.1
  7.2 0.0 all-gather.2.cloned.1.call-start
  7.2 2.2 pad_maximum_fusion.1
  9.4 0.0 all-gather.2.cloned.1.call-update
  9.4 154.0 %all-gather.2.cloned.1.call-done = bf16[1024,2880]{0,1:T(8,128)(2,1)} async-done(((bf16[128,2880]{0,1:T(8,128)(2,1)}), bf16[1024,2880]{0,1:T(8,128)(2,1)}) %all-gather.2.cloned.1.call-update) | async-done | bytes 5898256 | tf_op jit(solution)/shard_map/all_gather | solution.py:13
  163.4 2.2 fusion.21
  165.6 1.0 copy.8
  166.7 16.0 %all-to-all-start.1 = ((f32[8,16,960]{2,1,0:T(8,128)}), f32[8,16,960]{2,1,0:T(8,128)S(1)}, u32[]{:S(2)}, u32[]{:S(2)}) async-start(f32[8,16,960]{2,1,0:T(8,128)} %bitcast.4), calls=%async_computation.1 | async-start | bytes 1048576 | tf_op jit(solution)/shard_map/all_to_all | solution.py:24
  182.7 2.2 fusion.15
  184.9 2.2 fusion.18
  187.1 0.1 pad_maximum_fusion
  187.2 1.3 copy.7
  188.5 8.5 %all-to-all-done.1 = f32[8,16,960]{2,1,0:T(8,128)S(1)} async-done(((f32[8,16,960]{2,1,0:T(8,128)}), f32[8,16,960]{2,1,0:T(8,128)S(1)}, u32[]{:S(2)}, u32[]{:S(2)}) %all-to-all-start.1) | async-done | bytes 491552 | tf_op jit(solution)/shard_map/all_to_all | solution.py:24
  197.0 4.4 %all-to-all-start = ((f32[8,16,1920]{2,1,0:T(8,128)}), f32[8,16,1920]{2,1,0:T(8,128)S(1)}, u32[]{:S(2)}, u32[]{:S(2)}) async-start(f32[8,16,1920]{2,1,0:T(8,128)} %bitcast.2), calls=%async_computation | async-start | bytes 1966080 | tf_op jit(solution)/shard_map/all_to_all | solution.py:24
  201.5 24.2 %all-to-all-done = f32[8,16,1920]{2,1,0:T(8,128)S(1)} async-done(((f32[8,16,1920]{2,1,0:T(8,128)}), f32[8,16,1920]{2,1,0:T(8,128)S(1)}, u32[]{:S(2)}, u32[]{:S(2)}) %all-to-all-start) | async-done | bytes 983072 | tf_op jit(solution)/shard_map/all_to_all | solution.py:24
  225.7 0.1 reduce_sum.27
  225.7 0.1 multiply_convert_fusion.1
  225.8 0.7 broadcast_in_dim.7
  226.6 4.3 %all-to-all-start.3 = ((bf16[8,16,960]{2,1,0:T(8,128)(2,1)}), bf16[8,16,960]{2,1,0:T(8,128)(2,1)S(1)}, u32[]{:S(2)}, u32[]{:S(2)}) async-start(bf16[8,16,960]{2,1,0:T(8,128)(2,1)} %broadcast_in_dim.7), calls=%async_computation.3 | async-start | bytes 524288 | tf_op jit(solution)/shard_map/all_to_all | solution.py:53
  230.8 17.7 %all_gather.7 = bf16[128,960]{1,0:T(8,128)(2,1)S(1)} all-gather(bf16[16,960]{1,0:T(8,128)(2,1)S(1)} %get-tuple-element.4), channel_id=1, replica_groups=mesh['dp'=16,'tensor'=8,'section'=8] {'tensor'}, dimensions={0}, use_global_device_ids=true | all-gather | bytes 276480 | tf_op jit(solution)/shard_map/all_gather | solution.py:80
  248.5 0.0 all-to-all-done.3
  248.5 0.7 broadcast_in_dim.6
  249.3 3.5 %all-to-all-start.2 = ((bf16[8,16,960]{2,1,0:T(8,128)(2,1)}), bf16[8,16,960]{2,1,0:T(8,128)(2,1)S(1)}, u32[]{:S(2)}, u32[]{:S(2)}) async-start(bf16[8,16,960]{2,1,0:T(8,128)(2,1)} %broadcast_in_dim.6), calls=%async_computation.2 | async-start | bytes 524288 | tf_op jit(solution)/shard_map/all_to_all | solution.py:53
  252.7 2.0 fusion.2
  254.7 2.0 fusion.4
  256.7 4.7 %all-to-all-done.2 = bf16[8,16,960]{2,1,0:T(8,128)(2,1)S(1)} async-done(((bf16[8,16,960]{2,1,0:T(8,128)(2,1)}), bf16[8,16,960]{2,1,0:T(8,128)(2,1)S(1)}, u32[]{:S(2)}, u32[]{:S(2)}) %all-to-all-start.2) | async-done | bytes 245792 | tf_op jit(solution)/shard_map/all_to_all | solution.py:53
  261.4 2.0 fusion.12
  263.4 0.1 maximum_bitcast_fusion
  263.5 58.1 %all_to_all.25 = f32[16,8,2048]{2,1,0:T(8,128)S(1)} all-to-all(f32[16,8,2048]{2,1,0:T(8,128)S(1)} %maximum_bitcast_fusion), channel_id=1, replica_groups=mesh['dp'=16,'tensor'=8,'section'=8] {'dp'}, dimensions={0} | all-to-all | bytes 2097152 | tf_op jit(solution)/shard_map/all_to_all | solution.py:24
  321.6 0.1 reduce_sum.29
  321.7 0.6 fusion.24
  (3 shorter events, 0.0 us)
Async XLA Ops:
  7.2 175.5 %copy-start = (bf16[128,1024]{1,0:T(8,128)(2,1)S(1)}, bf16[128,1024]{1,0:T(8,128)(2,1)}, u32[]{:S(2)}) copy-start(bf16[128,1024]{1,0:T(8,128)(2,1)} %param.5) | copy-start | bytes 786436
  7.2 156.2 %copy-start.1 = (bf16[128,1024]{1,0:T(8,128)(2,1)S(1)}, bf16[128,1024]{1,0:T(8,128)(2,1)}, u32[]{:S(2)}) copy-start(bf16[128,1024]{1,0:T(8,128)(2,1)} %param.6) | copy-start | bytes 786436
  7.2 156.2 %all-gather.2.cloned.1.call-start = ((), (), s32[]{:S(2)}) async-start(), calls=%async_computation.5 | async-start | bytes 6635520 | tf_op jit(solution)/shard_map/all_gather | solution.py:13
  166.7 30.4 %all-to-all-start.1 = ((f32[8,16,960]{2,1,0:T(8,128)}), f32[8,16,960]{2,1,0:T(8,128)S(1)}, u32[]{:S(2)}, u32[]{:S(2)}) async-start(f32[8,16,960]{2,1,0:T(8,128)} %bitcast.4), calls=%async_computation.1 | async-start | bytes 1048576 | tf_op jit(solution)/shard_map/all_to_all | solution.py:24
  197.0 28.7 %all-to-all-start = ((f32[8,16,1920]{2,1,0:T(8,128)}), f32[8,16,1920]{2,1,0:T(8,128)S(1)}, u32[]{:S(2)}, u32[]{:S(2)}) async-start(f32[8,16,1920]{2,1,0:T(8,128)} %bitcast.2), calls=%async_computation | async-start | bytes 1966080 | tf_op jit(solution)/shard_map/all_to_all | solution.py:24
  226.6 22.0 %all-to-all-start.3 = ((bf16[8,16,960]{2,1,0:T(8,128)(2,1)}), bf16[8,16,960]{2,1,0:T(8,128)(2,1)S(1)}, u32[]{:S(2)}, u32[]{:S(2)}) async-start(bf16[8,16,960]{2,1,0:T(8,128)(2,1)} %broadcast_in_dim.7), calls=%async_computation.3 | async-start | bytes 524288 | tf_op jit(solution)/shard_map/all_to_all | solution.py:53
  249.3 12.2 %all-to-all-start.2 = ((bf16[8,16,960]{2,1,0:T(8,128)(2,1)}), bf16[8,16,960]{2,1,0:T(8,128)(2,1)S(1)}, u32[]{:S(2)}, u32[]{:S(2)}) async-start(bf16[8,16,960]{2,1,0:T(8,128)(2,1)} %broadcast_in_dim.6), calls=%async_computation.2 | async-start | bytes 524288 | tf_op jit(solution)/shard_map/all_to_all | solution.py:53
Sparse Core Ops, SparseCore 0:
  12.2 151.1 all-gather.1
where the time goes:
time: 335 us; the launch traced here: 329 us
  waiting for transfers between devices  191 us (57%)
  blocking collectives  75.7 us (23%)
  starting transfers between devices  28.2 us (8%)
  between operations  14.1 us (4%)
  matrix products  12.6 us (4%)
  local copies, waits for them, and re-layouts  4.42 us (1%)
    all_gather x1, waiting for transfers between devices, in_one_piece(): lax.all_gather(both, axis, axis=dim, tiled=True)  154 us
    all_to_all x1, blocking collectives, sent_and_summed(): lax.all_to_all(parts, axis, split_axis=0, concat_axis=0, tiled=True)  58.1 us
    all_to_all x2, waiting for transfers between devices, sent_and_summed(): lax.all_to_all(parts, axis, split_axis=0, concat_axis=0, tiled=True)  32.7 us
    all_to_all x2, starting transfers between devices, sent_and_summed(): lax.all_to_all(parts, axis, split_axis=0, concat_axis=0, tiled=True)  20.4 us
    all_gather x1, blocking collectives, body(): hidden = lax.all_gather(activate(gate, up), 'tensor', axis=0, tiled=True)  17.7 us
    all_to_all x2, starting transfers between devices, from_everyone(): return lax.all_to_all(copies, axis, split_axis=0, concat_axis=0, tiled=True)  7.75 us
  transfers between devices with their start and end apart: 5, of which 4 were waited for; matrix products, arithmetic and copies ran while one was open for 3% of the time, Pallas kernels for 0%

commit v1 on v0

v1 whole, which is shorter than its diff:
```python
import functools

import jax
import jax.numpy as jnp
from jax import lax
from jax.experimental import pallas as pl
from jax.experimental.pallas import tpu as pltpu
from jax.sharding import PartitionSpec as P

MESH = pl.DeviceIdType.MESH
CHUNKS = ((0, 256), (256, 256), (512, 256), (768, 192))
N = len(CHUNKS)
F32 = jnp.float32
BF16 = jnp.bfloat16
NT = (((1,), (1,)), ((), ()))


def kernel(*refs):
    refs = list(refs)

    def take(n):
        out = refs[:n]
        del refs[:n]
        return out

    tok, cot, gate_w, up_w, down_w = take(5)
    mixed_out, grad_out = take(2)
    (X,) = take(1)
    W, Pt, R, H = take(N), take(N), take(N), take(N)
    acc_m, acc_g, O, Q, O2, Z = take(6)
    x_send, x_recv = take(2)
    w_send, w_left, w_right, w_opp, w_pair = take(5)
    rs_send, rs_recv, ag_send, ag_recv = take(4)
    q_send, q_recv, z_send, z_recv = take(4)

    d = lax.axis_index("dp")
    t = lax.axis_index("tensor")
    s = lax.axis_index("section")
    yl, c = lax.div(t, 2), lax.rem(t, 2)
    x, h = lax.div(s, 2), lax.rem(s, 2)
    y = h * 4 + yl
    zh, zl = lax.div(d, 4), lax.rem(d, 4)

    pair = (d, 2 * yl + 1 - c, s)
    right = (d, t, lax.rem(x + 1, 4) * 2 + h)
    left = (d, t, lax.rem(x + 3, 4) * 2 + h)

    def along_y(q):
        return (d, 2 * lax.rem(q, 4) + c, x * 2 + lax.div(q, 4))

    def remote(src, dst, ss, rs, dev):
        return pltpu.make_async_remote_copy(
            src_ref=src, dst_ref=dst, send_sem=ss, recv_sem=rs, device_id=dev, device_id_type=MESH
        )

    def await_recv(ref, sem):
        remote(ref, ref, sem, sem, pair).wait_recv()

    def await_send(ref, sem):
        remote(ref, ref, sem, sem, pair).wait_send()

    own = pl.multiple_of(c * 512 + x * 128, 128)
    for f, (at, width) in enumerate(CHUNKS):
        for w, ref in enumerate((gate_w, up_w, down_w)):
            W[f][w, pl.ds(own, 128), :] = ref[:, at : at + width]

    barrier = pltpu.get_barrier_semaphore()
    partners = [pair, right, left, (d, 2 * yl + 1 - c, x * 2 + 1 - h)]
    partners += [along_y(lax.rem(y + k, 8)) for k in range(1, 8)]
    partners += [(zh * 4 + lax.rem(zl + k, 4), t, s) for k in range(1, 4)]
    for k in range(1, 4):
        far = lax.rem(zh + k, 4) * 4 + zl
        partners += [(far, 2 * yl + a, x * 2 + b) for a in range(2) for b in range(2)]
    for p in partners:
        pl.semaphore_signal(barrier, inc=1, device_id=p, device_id_type=MESH)
    pl.semaphore_wait(barrier, len(partners))

    def rows(core, at, size=128, extra=0):
        return pl.ds(pl.multiple_of(core * 512 + lax.rem(at, 4) * 128 + extra, 64), size)

    def start_own(f):
        mine = W[f].at[:, rows(c, x), :]
        remote(mine, mine, w_send.at[f], w_left.at[f], right).start()
        remote(mine, mine, w_send.at[f], w_right.at[f], left).start()
        remote(mine, mine, w_send.at[f], w_pair.at[f], pair).start()

    start_own(0)

    for a, ref in enumerate((tok, cot)):
        for other in range(2):
            to = lax.rem(h + other, 2)
            for b in range(4):
                src = ref.at[:, pl.ds(pl.multiple_of((b * 2 + to) * 128, 128), 128)]
                dst = X.at[a, :, pl.ds(pl.multiple_of(c * 512 + b * 128, 128), 128)]
                dev = (d, 2 * yl + h, x * 2 + to)
                if other:
                    remote(src, dst, x_send, x_recv, dev).start()
                else:

                    @pl.when(c == h)
                    def _():
                        pltpu.make_async_copy(src, dst, x_recv).start()

                    @pl.when(c != h)
                    def _():
                        remote(src, dst, x_send, x_recv, dev).start()

    start_own(1)
    acc_m[...] = jnp.zeros_like(acc_m)
    acc_g[...] = jnp.zeros_like(acc_g)

    def gather(f):
        fl = W[f].at[:, rows(c, x + 3), :]
        await_recv(fl, w_left.at[f])
        half = W[f].at[:, rows(c, x + 3, 64), :]
        remote(half, half, w_send.at[f], w_opp.at[f], right).start()
        remote(fl, fl, w_send.at[f], w_pair.at[f], pair).start()
        fr = W[f].at[:, rows(c, x + 1), :]
        await_recv(fr, w_right.at[f])
        half = W[f].at[:, rows(c, x + 1, 64, 64), :]
        remote(half, half, w_send.at[f], w_opp.at[f], left).start()
        remote(fr, fr, w_send.at[f], w_pair.at[f], pair).start()
        if f + 2 < N:
            start_own(f + 2)
        fo = W[f].at[:, rows(c, x + 2), :]
        await_recv(fo, w_opp.at[f])
        remote(fo, fo, w_send.at[f], w_pair.at[f], pair).start()
        await_recv(W[f].at[:, pl.ds(0, 512), :], w_pair.at[f])

    def partial_sums(f):
        width = CHUNKS[f][1]
        for w in range(3):
            part = jnp.dot(X[w // 2], W[f][w], preferred_element_type=F32)
            Pt[f][:, w, :, :] = part.astype(BF16).reshape(8, 16, width)
        for k in range(1, 8):
            q = lax.rem(y + k, 8)
            remote(
                Pt[f].at[q], R[f].at[k - 1], rs_send.at[f], rs_recv.at[f], along_y(q)
            ).start()

    def activate(f):
        await_recv(R[f], rs_recv.at[f])
        total = [Pt[f][y, w].astype(F32) for w in range(3)]
        for k in range(7):
            for w in range(3):
                total[w] = total[w] + R[f][k, w].astype(F32)
        gate, up, back = total
        sig = 1.0 / (1.0 + jnp.exp(-gate))
        H[f][y, 0] = (gate * sig * up).astype(BF16)
        H[f][y, 1] = (back * up * sig * (1.0 + gate * (1.0 - sig))).astype(BF16)
        H[f][y, 2] = (back * gate * sig).astype(BF16)
        for k in range(1, 8):
            mine = H[f].at[y]
            remote(
                mine, mine, ag_send.at[f], ag_recv.at[f], along_y(lax.rem(y + k, 8))
            ).start()

    def outputs(f):
        width = CHUNKS[f][1]
        await_recv(H[f].at[pl.ds(0, 7)], ag_recv.at[f])
        hid, gg, ug = (H[f][:, w].reshape(128, width) for w in range(3))
        acc_m[...] += lax.dot_general(hid, W[f][2], NT, preferred_element_type=F32)
        acc_g[...] += lax.dot_general(
            gg, W[f][0], NT, preferred_element_type=F32
        ) + lax.dot_general(ug, W[f][1], NT, preferred_element_type=F32)

    for step in range(N + 2):
        if step < N:
            gather(step)
            if step == 0:
                await_recv(X, x_recv)
            partial_sums(step)
        if 0 <= step - 1 < N:
            activate(step - 1)
        if 0 <= step - 2:
            outputs(step - 2)

    for e in range(16):
        for v in range(2):
            O[e % 4, e // 4, v, :, 0:512] = acc_m[
                e * 8 : e * 8 + 8, v * 512 : v * 512 + 512
            ].astype(BF16)
            O[e % 4, e // 4, v, :, 512:1024] = acc_g[
                e * 8 : e * 8 + 8, v * 512 : v * 512 + 512
            ].astype(BF16)
    for k in range(1, 4):
        to = lax.rem(zl + k, 4)
        remote(O.at[to], Q.at[k - 1], q_send, q_recv, (zh * 4 + to, t, s)).start()
    await_recv(Q, q_recv)
    for e in range(4):
        for v in range(2):
            part = O[zl, e, v].astype(F32)
            for k in range(3):
                part = part + Q[k, e, v].astype(F32)
            O2[e, v] = part.astype(BF16)
    for k in range(4):
        to = lax.rem(zh + k, 4)
        for v in range(2):
            src, dst = O2.at[to, v], Z.at[h * 4 + zh]
            dev = (to * 4 + zl, 2 * yl + v, x * 2 + c)
            if k:
                remote(src, dst, z_send, z_recv, dev).start()
            else:
                mine = jnp.logical_and(c == h, c == v)

                @pl.when(mine)
                def _():
                    pltpu.make_async_copy(src, dst, z_recv).start()

                @pl.when(jnp.logical_not(mine))
                def _():
                    remote(src, dst, z_send, z_recv, dev).start()

    await_recv(Z, z_recv)
    for b in range(2):
        total = Z[b * 4].astype(F32)
        for k in range(1, 4):
            total = total + Z[b * 4 + k].astype(F32)
        for a in range(4):
            to = (a * 2 + b) * 128
            mixed_out[:, to : to + 128] = total[:, a * 128 : a * 128 + 128].astype(BF16)
            grad_out[:, to : to + 128] = total[:, 512 + a * 128 : 640 + a * 128].astype(BF16)

    for f in range(N):
        await_send(W[f].at[:, pl.ds(0, 896), :], w_send.at[f])
        await_send(R[f], rs_send.at[f])
        await_send(H[f].at[pl.ds(0, 7)], ag_send.at[f])
    await_send(Q, q_send)

    @pl.when(c == h)
    def _():
        await_send(X.at[:, :, pl.ds(0, 512)], x_send)
        await_send(Z.at[pl.ds(0, 7)], z_send)

    @pl.when(c != h)
    def _():
        await_send(X, x_send)
        await_send(Z, z_send)


def body(*args):
    dma = pltpu.SemaphoreType.DMA
    widths = [w for _, w in CHUNKS]
    scratch = [pltpu.VMEM((2, 128, 1024), BF16)]
    scratch += [pltpu.VMEM((3, 1024, w), BF16) for w in widths]
    scratch += [pltpu.VMEM((8, 3, 16, w), BF16) for w in widths]
    scratch += [pltpu.VMEM((7, 3, 16, w), BF16) for w in widths]
    scratch += [pltpu.VMEM((8, 3, 16, w), BF16) for w in widths]
    scratch += [
        pltpu.VMEM((128, 1024), F32),
        pltpu.VMEM((128, 1024), F32),
        pltpu.VMEM((4, 4, 2, 8, 1024), BF16),
        pltpu.VMEM((3, 4, 2, 8, 1024), BF16),
        pltpu.VMEM((4, 2, 8, 1024), BF16),
        pltpu.VMEM((8, 8, 1024), BF16),
    ]
    scratch += [dma, dma]
    scratch += [dma((N,))] * 5
    scratch += [dma((N,))] * 4
    scratch += [dma] * 4
    vmem = pl.BlockSpec(memory_space=pltpu.VMEM)
    return pl.pallas_call(
        kernel,
        out_shape=[jax.ShapeDtypeStruct((8, 1024), BF16)] * 2,
        in_specs=[vmem] * 5,
        out_specs=[vmem] * 2,
        scratch_shapes=scratch,
        compiler_params=pltpu.CompilerParams(collective_id=0, has_side_effects=True),
        name="ffn",
    )(*args)


def solution(mesh):
    placed = (
        P("section", "tensor"),
        P("section", "tensor"),
        P(("tensor", "section"), "dp"),
        P(("tensor", "section"), "dp"),
        P(("tensor", "section"), "dp"),
    )
    return jax.shard_map(
        lambda *args: tuple(body(*args)),
        mesh=mesh,
        in_specs=placed,
        out_specs=(P(("section", "dp"), "tensor"), P(("section", "dp"), "tensor")),
        check_vma=False,
    )
```

time: 335 us -> 115 us (0.34)
  the two profiles are of different devices: /device:TPU:1 before, /device:TPU:3 now
where the time goes in v1:
time: 115 us; the launch traced here: 114 us
  Pallas kernels  108 us (94%)
  local copies, waits for them, and re-layouts  5.54 us (5%)
    pallas_call x1, Pallas kernels, body(): pl.pallas_call(kernel, out_shape=[jax.ShapeDtypeStruct((8, 1024), BF16)]...  108 us
    unnamed x11, local copies, waits for them, and re-layouts  5.54 us

profile of v1, /device:TPU:3, one launch (start us, length us, event | category | flops | bytes accessed | tf_op | source)
XLA Modules:
  0.0 114.5 jit_solution(11278404953911823259)
XLA Ops:
  0.6 0.0 copy-start
  0.6 1.8 %copy.7.refs_2_ = bf16[128,960]{1,0:T(8,128)(2,1)} copy(bf16[128,960]{0,1:T(8,128)(2,1)} %param.7) | data formatting | bytes 491520 | tf_op args[2]
  2.5 0.0 copy-done
  2.5 0.0 copy-start.1
  2.5 0.8 copy.8.refs_3_
  3.3 0.1 copy-done.1
  3.4 0.8 copy.9.refs_4_
  4.2 108.3 %ffn.1 = (bf16[8,1024]{1,0:T(8,128)(2,1)}, bf16[8,1024]{1,0:T(8,128)(2,1)}) custom-call(bf16[128,1024]{1,0:T(8,128)(2,1)} %refs_0_.1, bf16[128,1024]{1,0:T(8,128)(2,1)} %refs_1_.1, bf16[128,960]{1,0:T(8,128)(2,1)} %copy.7.refs_2_, bf16[128,960]{1,0:T(8,128)(2,1)} %copy.8.refs_3_, bf16[128,960]{1,0:T(8,128)(2,1)} %copy.9.refs_4_), custom_call_target="tpu_custom_call" | custom-call | tf_op jit(solution)/shard_map/ffn/pallas_call | solution.py:262
  112.5 0.0 copy-start.2
  112.5 1.3 %copy.12 = bf16[8,1024]{1,0:T(8,128)(2,1)} copy(bf16[8,1024]{1,0:T(8,128)(2,1)} %get-tuple-element.4) | data formatting | bytes 32768
  113.9 0.0 copy-done.2
  113.9 0.6 copy.13
Async XLA Ops:
  0.6 1.8 %copy-start = (bf16[128,960]{0,1:T(8,128)(2,1)S(1)}, bf16[128,960]{0,1:T(8,128)(2,1)}, u32[]{:S(2)}) copy-start(bf16[128,960]{0,1:T(8,128)(2,1)} %param.8) | copy-start | bytes 737284
  2.5 0.9 copy-start.1
  112.5 1.3 %copy-start.2 = (bf16[8,1024]{1,0:T(8,128)(2,1)S(1)}, bf16[8,1024]{1,0:T(8,128)(2,1)}, u32[]{:S(2)}) copy-start(bf16[8,1024]{1,0:T(8,128)(2,1)} %get-tuple-element.5) | copy-start | bytes 49156

commit v2 on v0

v2 whole, which is shorter than its diff:
```python
import jax
import jax.numpy as jnp
from jax import lax
from jax.experimental import pallas as pl
from jax.experimental.pallas import tpu as pltpu
from jax.sharding import PartitionSpec as P

MESH = pl.DeviceIdType.MESH
CHUNKS = ((0, 256), (256, 256), (512, 256), (768, 192))
N = len(CHUNKS)
UNITS = [("gu", f) for f in range(N)] + [("dn", f) for f in range(N)]
M = len(UNITS)
GU = [UNITS.index(("gu", f)) for f in range(N)]
DN = [UNITS.index(("dn", f)) for f in range(N)]
HOW_MANY = [2 if kind == "gu" else 1 for kind, _ in UNITS]
GATHERED = [1 if kind == "gu" else 2 for kind, _ in UNITS]
WIDTH = [CHUNKS[f][1] for _, f in UNITS]
F32 = jnp.float32
BF16 = jnp.bfloat16
NT = (((1,), (1,)), ((), ()))


def kernel(*refs):
    refs = list(refs)

    def take(n):
        out = refs[:n]
        del refs[:n]
        return out

    tok, cot, gate_w, up_w, down_w = take(5)
    mixed_out, grad_out = take(2)
    T, X = take(2)
    W, Pt, Pf, R, H = take(M), take(M), take(M), take(M), take(M)
    G = take(N)
    acc_m, acc_g, O, Q, O2, Z = take(6)
    t_load, w_load = take(2)
    x_send, x_recv = take(2)
    w_send, w_left, w_right, w_opp, w_pair = take(5)
    rs_send, rs_recv, ag_send, ag_recv = take(4)
    q_send, q_recv, z_send, z_recv = take(4)

    d = lax.axis_index("dp")
    t = lax.axis_index("tensor")
    s = lax.axis_index("section")
    yl, c = lax.div(t, 2), lax.rem(t, 2)
    x, h = lax.div(s, 2), lax.rem(s, 2)
    y = h * 4 + yl
    zh, zl = lax.div(d, 4), lax.rem(d, 4)

    pair = (d, 2 * yl + 1 - c, s)
    right = (d, t, lax.rem(x + 1, 4) * 2 + h)
    left = (d, t, lax.rem(x + 3, 4) * 2 + h)

    def along_y(q):
        return (d, 2 * lax.rem(q, 4) + c, x * 2 + lax.div(q, 4))

    def remote(src, dst, ss, rs, dev):
        return pltpu.make_async_remote_copy(
            src_ref=src, dst_ref=dst, send_sem=ss, recv_sem=rs, device_id=dev, device_id_type=MESH
        )

    def await_recv(ref, sem):
        remote(ref, ref, sem, sem, pair).wait_recv()

    def await_send(ref, sem):
        remote(ref, ref, sem, sem, pair).wait_send()

    def block(at):
        return c * 4 + lax.rem(at, 4)

    def lanes(at):
        return pl.ds(pl.multiple_of(at, 128), 128)

    for u, (kind, f) in enumerate(UNITS):
        at, width = CHUNKS[f]
        for w, ref in enumerate((gate_w, up_w) if kind == "gu" else (down_w,)):
            pltpu.make_async_copy(
                ref.at[pl.ds(at, width), :], W[u].at[w, block(x)], w_load.at[u]
            ).start()
        if u == 0:
            for a, ref in enumerate((tok, cot)):
                pltpu.make_async_copy(ref, T.at[a], t_load).start()

    @pl.when(c == h)
    def _():
        for a, ref in enumerate((tok, cot)):
            for b in range(4):
                pltpu.make_async_copy(
                    ref.at[:, lanes((b * 2 + h) * 128)],
                    X.at[a, :, lanes(c * 512 + b * 128)],
                    x_recv,
                ).start()

    barrier = pltpu.get_barrier_semaphore()
    partners = [pair, right, left, (d, 2 * yl + 1 - c, x * 2 + 1 - h)]
    partners += [along_y(lax.rem(y + k, 8)) for k in range(1, 8)]
    partners += [(zh * 4 + lax.rem(zl + k, 4), t, s) for k in range(1, 4)]
    for k in range(1, 4):
        far = lax.rem(zh + k, 4) * 4 + zl
        partners += [(far, 2 * yl + a, x * 2 + b) for a in range(2) for b in range(2)]
    for p in partners:
        pl.semaphore_signal(barrier, inc=1, device_id=p, device_id_type=MESH)
    acc_m[...] = jnp.zeros_like(acc_m)
    acc_g[...] = jnp.zeros_like(acc_g)
    pl.semaphore_wait(barrier, len(partners))

    def start_own(u):
        mine = W[u].at[:, block(x)]
        pltpu.make_async_copy(mine, mine, w_load.at[u]).wait()
        remote(mine, mine, w_send.at[u], w_left.at[u], right).start()
        remote(mine, mine, w_send.at[u], w_right.at[u], left).start()
        remote(mine, mine, w_send.at[u], w_pair.at[u], pair).start()

    start_own(0)

    pltpu.make_async_copy(T, T, t_load).wait()
    for other in (1, 0):
        to = lax.rem(h + other, 2)
        dev = (d, 2 * yl + h, x * 2 + to)

        def spread():
            for a in range(2):
                for b in range(4):
                    remote(
                        T.at[a, :, lanes((b * 2 + to) * 128)],
                        X.at[a, :, lanes(c * 512 + b * 128)],
                        x_send,
                        x_recv,
                        dev,
                    ).start()

        if other:
            spread()
        else:
            pl.when(c != h)(spread)

    start_own(1)

    def take_neighbours(u):
        half = WIDTH[u] // 2
        got = W[u].at[:, block(x + 3)]
        await_recv(got, w_left.at[u])
        some = W[u].at[:, block(x + 3), pl.ds(0, half)]
        remote(some, some, w_send.at[u], w_opp.at[u], right).start()
        remote(got, got, w_send.at[u], w_pair.at[u], pair).start()
        got = W[u].at[:, block(x + 1)]
        await_recv(got, w_right.at[u])
        some = W[u].at[:, block(x + 1), pl.ds(half, half)]
        remote(some, some, w_send.at[u], w_opp.at[u], left).start()
        remote(got, got, w_send.at[u], w_pair.at[u], pair).start()
        for v in {2: (4, 5)}.get(u, (u + 2 if u < 2 else u + 3,)):
            if v < M:
                start_own(v)

    def take_opposite(u):
        got = W[u].at[:, block(x + 2)]
        await_recv(got, w_opp.at[u])
        remote(got, got, w_send.at[u], w_pair.at[u], pair).start()
        await_recv(W[u].at[:, pl.ds(0, 4)], w_pair.at[u])

    def weight(u, w):
        return jnp.concatenate([W[u][w, b] for b in range(8)], axis=1)

    def partial_sums(u):
        kind, width = UNITS[u][0], WIDTH[u]
        rows = X[0 if kind == "gu" else 1]
        for w in range(HOW_MANY[u]):
            part = lax.dot_general(rows, weight(u, w), NT, preferred_element_type=F32)
            Pf[u][:, w] = part.reshape(8, 16, width)
            Pt[u][:, w] = part.astype(BF16).reshape(8, 16, width)
        for k in (4, 3, 5, 2, 6, 1, 7):
            q = lax.rem(y + k, 8)
            remote(
                Pt[u].at[q], R[u].at[k - 1], rs_send.at[u], rs_recv.at[u], along_y(q)
            ).start()

    def activate(u):
        kind, f = UNITS[u]
        await_recv(R[u], rs_recv.at[u])
        total = [Pf[u][y, w] for w in range(HOW_MANY[u])]
        for k in range(7):
            for w in range(HOW_MANY[u]):
                total[w] = total[w] + R[u][k, w].astype(F32)
        if kind == "gu":
            gate, up = total
            G[f][0], G[f][1] = gate, up
            sig = 1.0 / (1.0 + jnp.exp(-gate))
            H[u][y, 0] = (gate * sig * up).astype(BF16)
        else:
            (back,) = total
            gate, up = G[f][0], G[f][1]
            sig = 1.0 / (1.0 + jnp.exp(-gate))
            H[u][y, 0] = (back * up * sig * (1.0 + gate * (1.0 - sig))).astype(BF16)
            H[u][y, 1] = (back * gate * sig).astype(BF16)
        mine = H[u].at[y]
        for k in (4, 3, 5, 2, 6, 1, 7):
            remote(
                mine, mine, ag_send.at[u], ag_recv.at[u], along_y(lax.rem(y + k, 8))
            ).start()

    def mix(f):
        u = GU[f]
        await_recv(H[u].at[pl.ds(0, 7)], ag_recv.at[u])
        hid = H[u][:, 0].reshape(128, WIDTH[u])
        acc_m[...] += jnp.dot(hid, weight(DN[f], 0), preferred_element_type=F32)

    def grads(f):
        u = DN[f]
        await_recv(H[u].at[pl.ds(0, 7)], ag_recv.at[u])
        gg, ug = (H[u][:, w].reshape(128, WIDTH[u]) for w in range(2))
        acc_g[...] += jnp.dot(gg, weight(GU[f], 0), preferred_element_type=F32) + jnp.dot(
            ug, weight(GU[f], 1), preferred_element_type=F32
        )

    accs, outs = (acc_m, acc_g), (mixed_out, grad_out)

    def near_start(a):
        for e in range(16):
            for v in range(2):
                O[a, e % 4, e // 4, v] = accs[a][
                    e * 8 : e * 8 + 8, v * 512 : v * 512 + 512
                ].astype(BF16)
        for k in (3, 2, 1):
            to = lax.rem(zl + k, 4)
            remote(
                O.at[a, to], Q.at[a, k - 1], q_send.at[a], q_recv.at[a], (zh * 4 + to, t, s)
            ).start()

    def far_start(a):
        await_recv(Q.at[a], q_recv.at[a])
        for e in range(4):
            for v in range(2):
                part = accs[a][
                    pl.ds(pl.multiple_of(e * 32 + zl * 8, 8), 8), v * 512 : v * 512 + 512
                ]
                for k in range(3):
                    part = part + Q[a, k, e, v].astype(F32)
                O2[a, e, v] = part.astype(BF16)
        for k in (2, 1, 3, 0):
            to = lax.rem(zh + k, 4)
            for v in range(2):
                src, dst = O2.at[a, to, v], Z.at[a, h * 4 + zh]
                dev = (to * 4 + zl, 2 * yl + v, x * 2 + c)
                if k:
                    remote(src, dst, z_send.at[a], z_recv.at[a], dev).start()
                else:
                    mine = jnp.logical_and(c == h, c == v)

                    @pl.when(mine)
                    def _():
                        pltpu.make_async_copy(src, dst, z_recv.at[a]).start()

                    @pl.when(jnp.logical_not(mine))
                    def _():
                        remote(src, dst, z_send.at[a], z_recv.at[a], dev).start()

    def finish(a):
        await_recv(Z.at[a], z_recv.at[a])
        for b in range(2):
            total = Z[a, b * 4].astype(F32)
            for k in range(1, 4):
                total = total + Z[a, b * 4 + k].astype(F32)
            for e in range(4):
                to = (e * 2 + b) * 128
                outs[a][:, to : to + 128] = total[:, e * 128 : e * 128 + 128].astype(BF16)

    take_neighbours(0)
    for i in range(M + 2):
        if i + 1 < M:
            take_neighbours(i + 1)
        if i < M:
            take_opposite(i)
            if i == 0:
                await_recv(X, x_recv)
            partial_sums(i)
        if i >= 2:
            activate(i - 2)
        if i < M and UNITS[i][0] == "dn":
            mix(UNITS[i][1])
            if i == M - 1:
                near_start(0)
        if i >= 4 and UNITS[i - 4][0] == "dn":
            grads(UNITS[i - 4][1])
    far_start(0)
    grads(UNITS[M - 2][1])
    grads(UNITS[M - 1][1])
    near_start(1)
    far_start(1)
    finish(0)
    finish(1)

    for u in range(M):
        await_send(W[u].at[:, pl.ds(0, 7)], w_send.at[u])
        await_send(R[u], rs_send.at[u])
        await_send(H[u].at[pl.ds(0, 7)], ag_send.at[u])
    for a in range(2):
        await_send(Q.at[a], q_send.at[a])

    @pl.when(c == h)
    def _():
        await_send(X.at[:, :, pl.ds(0, 512)], x_send)
        for a in range(2):
            await_send(Z.at[a, pl.ds(0, 7)], z_send.at[a])

    @pl.when(c != h)
    def _():
        await_send(X, x_send)
        for a in range(2):
            await_send(Z.at[a], z_send.at[a])


def body(tokens, cotangent, gate_weight, up_weight, down_weight):
    dma = pltpu.SemaphoreType.DMA
    vmem = pltpu.VMEM
    scratch = [vmem((2, 128, 1024), BF16)] * 2
    units = list(zip(HOW_MANY, GATHERED, WIDTH))
    scratch += [vmem((n, 8, w, 128), BF16) for n, _, w in units]
    scratch += [vmem((8, n, 16, w), BF16) for n, _, w in units]
    scratch += [vmem((8, n, 16, w), F32) for n, _, w in units]
    scratch += [vmem((7, n, 16, w), BF16) for n, _, w in units]
    scratch += [vmem((8, n, 16, w), BF16) for _, n, w in units]
    scratch += [vmem((2, 16, w), F32) for _, w in CHUNKS]
    scratch += [
        vmem((128, 1024), F32),
        vmem((128, 1024), F32),
        vmem((2, 4, 4, 2, 8, 512), BF16),
        vmem((2, 3, 4, 2, 8, 512), BF16),
        vmem((2, 4, 2, 8, 512), BF16),
        vmem((2, 8, 8, 512), BF16),
    ]
    scratch += [dma, dma((M,)), dma, dma]
    scratch += [dma((M,))] * 5
    scratch += [dma((M,))] * 4
    scratch += [dma((2,))] * 4
    return pl.pallas_call(
        kernel,
        out_shape=[jax.ShapeDtypeStruct((8, 1024), BF16)] * 2,
        in_specs=[pl.BlockSpec(memory_space=pl.ANY)] * 5,
        out_specs=[pl.BlockSpec(memory_space=pltpu.VMEM)] * 2,
        scratch_shapes=scratch,
        compiler_params=pltpu.CompilerParams(collective_id=0, has_side_effects=True),
        name="ffn",
    )(tokens, cotangent, gate_weight.T, up_weight.T, down_weight.T)


def solution(mesh):
    placed = (
        P("section", "tensor"),
        P("section", "tensor"),
        P(("tensor", "section"), "dp"),
        P(("tensor", "section"), "dp"),
        P(("tensor", "section"), "dp"),
    )
    return jax.shard_map(
        lambda *args: tuple(body(*args)),
        mesh=mesh,
        in_specs=placed,
        out_specs=(P(("section", "dp"), "tensor"), P(("section", "dp"), "tensor")),
        check_vma=False,
    )
```

time: 335 us -> 100 us (0.30); the launches traced: 329 us -> 100 us
  waiting for transfers between devices: 191 us -> 0 us
  Pallas kernels: 0 us -> 97.4 us
  blocking collectives: 75.7 us -> 0 us
  starting transfers between devices: 28.2 us -> 0 us
  between operations: 14.1 us -> 0.65 us
  matrix products: 12.6 us -> 0 us
    all_gather x1 -> x0, waiting for transfers between devices: 154 us -> none  [in_one_piece(): lax.all_gather(both, axis, axis=dim, tiled=True)]
    pallas_call x0 -> x1, Pallas kernels: none -> 97.4 us  [body(): pl.pallas_call(kernel, out_shape=[jax.ShapeDtypeStruct((8, 1024), BF16)]...]
    all_to_all x1 -> x0, blocking collectives: 58.1 us -> none  [sent_and_summed(): lax.all_to_all(parts, axis, split_axis=0, concat_axis=0, tiled=True)]
    all_to_all x4 -> x0, waiting for transfers between devices: 37.4 us -> none  [the longest x2 32.7 us: sent_and_summed(): lax.all_to_all(parts, axis, split_axis=0, concat_axis=0, tiled=True)]
    all_to_all x4 -> x0, starting transfers between devices: 28.2 us -> none  [the longest x2 20.4 us: sent_and_summed(): lax.all_to_all(parts, axis, split_axis=0, concat_axis=0, tiled=True)]
    all_gather x1 -> x0, blocking collectives: 17.7 us -> none  [body(): hidden = lax.all_gather(activate(gate, up), 'tensor', axis=0, tiled=True)]
    dot_general x6 -> x0, matrix products: 12.6 us -> none  [the longest x1 2.22 us: body(): up_part = jnp.dot(tokens, up_new, preferred_element_type=jnp.float32)]
  transfers between devices with their start and end apart: 5 -> 0, of which waited for: 4 -> 0; matrix products, arithmetic and copies ran while one was open for 3% -> 0% of each run, Pallas kernels for 0% -> 0%
where the time goes in v2:
time: 100 us
  Pallas kernels  97.4 us (97%)
  local copies, waits for them, and re-layouts  1.94 us (2%)
    pallas_call x1, Pallas kernels, body(): pl.pallas_call(kernel, out_shape=[jax.ShapeDtypeStruct((8, 1024), BF16)]...  97.4 us

profile of v2, /device:TPU:1, one launch (start us, length us, event | category | flops | bytes accessed | tf_op | source)
XLA Modules:
  0.0 100.0 jit_solution(6062053780710757674)
XLA Ops:
  0.6 97.4 %ffn.1 = (bf16[8,1024]{1,0:T(8,128)(2,1)}, bf16[8,1024]{1,0:T(8,128)(2,1)}) custom-call(bf16[128,1024]{1,0:T(8,128)(2,1)} %refs_0_.1, bf16[128,1024]{1,0:T(8,128)(2,1)} %refs_1_.1, bf16[960,128]{1,0:T(8,128)(2,1)} %bitcast.3, bf16[960,128]{1,0:T(8,128)(2,1)} %bitcast.4, bf16[960,128]{1,0:T(8,128)(2,1)} %bitcast.5), custom_call_target="tpu_custom_call" | custom-call | tf_op jit(solution)/shard_map/ffn/pallas_call | solution.py:336
  98.0 0.0 copy-start
  98.0 1.3 %copy.9 = bf16[8,1024]{1,0:T(8,128)(2,1)} copy(bf16[8,1024]{1,0:T(8,128)(2,1)} %get-tuple-element.4) | data formatting | bytes 32768
  99.3 0.0 copy-done
  99.3 0.6 copy.10
Async XLA Ops:
  98.0 1.3 %copy-start = (bf16[8,1024]{1,0:T(8,128)(2,1)S(1)}, bf16[8,1024]{1,0:T(8,128)(2,1)}, u32[]{:S(2)}) copy-start(bf16[8,1024]{1,0:T(8,128)(2,1)} %get-tuple-element.5) | copy-start | bytes 49156

commit v3 on v2

--- a/solution.py
+++ b/solution.py
@@ -6,7 +6,7 @@
 from jax.sharding import PartitionSpec as P
 
 MESH = pl.DeviceIdType.MESH
-CHUNKS = ((0, 256), (256, 256), (512, 256), (768, 192))
+CHUNKS = ((0, 192), (192, 256), (448, 256), (704, 256))
 N = len(CHUNKS)
 UNITS = [("gu", f) for f in range(N)] + [("dn", f) for f in range(N)]
 M = len(UNITS)
@@ -18,6 +18,8 @@
 F32 = jnp.float32
 BF16 = jnp.bfloat16
 NT = (((1,), (1,)), ((), ()))
+REACH = (1, 2, 4, 1)
+FAR_FIRST = (8, 7, 9, 6, 10, 5, 11, 4, 12, 3, 13, 2, 14, 1, 15, 0)
 
 
 def kernel(*refs):
@@ -33,12 +35,12 @@
     T, X = take(2)
     W, Pt, Pf, R, H = take(M), take(M), take(M), take(M), take(M)
     G = take(N)
-    acc_m, acc_g, O, Q, O2, Z = take(6)
+    acc_m, acc_g, O, Z = take(4)
     t_load, w_load = take(2)
     x_send, x_recv = take(2)
     w_send, w_left, w_right, w_opp, w_pair = take(5)
-    rs_send, rs_recv, ag_send, ag_recv = take(4)
-    q_send, q_recv, z_send, z_recv = take(4)
+    rs_send, rs_recv, ag_send, ag_recv, ag_low, ag_high = take(6)
+    z_send, z_recv, ready = take(3)
 
     d = lax.axis_index("dp")
     t = lax.axis_index("tensor")
@@ -46,7 +48,6 @@
     yl, c = lax.div(t, 2), lax.rem(t, 2)
     x, h = lax.div(s, 2), lax.rem(s, 2)
     y = h * 4 + yl
-    zh, zl = lax.div(d, 4), lax.rem(d, 4)
 
     pair = (d, 2 * yl + 1 - c, s)
     right = (d, t, lax.rem(x + 1, 4) * 2 + h)
@@ -89,21 +90,26 @@
                 pltpu.make_async_copy(
                     ref.at[:, lanes((b * 2 + h) * 128)],
                     X.at[a, :, lanes(c * 512 + b * 128)],
-                    x_recv,
+                    x_recv.at[a],
                 ).start()
 
     barrier = pltpu.get_barrier_semaphore()
-    partners = [pair, right, left, (d, 2 * yl + 1 - c, x * 2 + 1 - h)]
-    partners += [along_y(lax.rem(y + k, 8)) for k in range(1, 8)]
-    partners += [(zh * 4 + lax.rem(zl + k, 4), t, s) for k in range(1, 4)]
-    for k in range(1, 4):
-        far = lax.rem(zh + k, 4) * 4 + zl
-        partners += [(far, 2 * yl + a, x * 2 + b) for a in range(2) for b in range(2)]
+    partners = [along_y(lax.rem(y + k, 8)) for k in (4, 3, 5, 2, 6, 1, 7)]
+    partners += [(d, 2 * yl + 1 - c, x * 2 + 1 - h), right, left, pair]
+    partners += [(lax.rem(d + k, 16), t, s) for k in (1, 15)]
     for p in partners:
         pl.semaphore_signal(barrier, inc=1, device_id=p, device_id_type=MESH)
     acc_m[...] = jnp.zeros_like(acc_m)
     acc_g[...] = jnp.zeros_like(acc_g)
     pl.semaphore_wait(barrier, len(partners))
+
+    def tell(r):
+        for k in (REACH[r], 16 - REACH[r]):
+            pl.semaphore_signal(
+                ready.at[r], inc=1, device_id=(lax.rem(d + k, 16), t, s), device_id_type=MESH
+            )
+
+    tell(0)
 
     def start_own(u):
         mine = W[u].at[:, block(x)]
@@ -115,25 +121,25 @@
     start_own(0)
 
     pltpu.make_async_copy(T, T, t_load).wait()
-    for other in (1, 0):
-        to = lax.rem(h + other, 2)
-        dev = (d, 2 * yl + h, x * 2 + to)
-
-        def spread():
-            for a in range(2):
+    for a in range(2):
+        for other in (1, 0):
+            to = lax.rem(h + other, 2)
+            dev = (d, 2 * yl + h, x * 2 + to)
+
+            def spread():
                 for b in range(4):
                     remote(
                         T.at[a, :, lanes((b * 2 + to) * 128)],
                         X.at[a, :, lanes(c * 512 + b * 128)],
                         x_send,
-                        x_recv,
+                        x_recv.at[a],
                         dev,
                     ).start()
 
-        if other:
-            spread()
-        else:
-            pl.when(c != h)(spread)
+            if other:
+                spread()
+            else:
+                pl.when(c != h)(spread)
 
     start_own(1)
 
@@ -194,20 +200,38 @@
             H[u][y, 0] = (back * up * sig * (1.0 + gate * (1.0 - sig))).astype(BF16)
             H[u][y, 1] = (back * gate * sig).astype(BF16)
         mine = H[u].at[y]
-        for k in (4, 3, 5, 2, 6, 1, 7):
+        for k, sem in ((2, ag_low), (6, ag_high), (1, ag_recv), (7, ag_recv)):
             remote(
-                mine, mine, ag_send.at[u], ag_recv.at[u], along_y(lax.rem(y + k, 8))
+                mine, mine, ag_send.at[u], sem.at[u], along_y(lax.rem(y + k, 8))
             ).start()
+
+    def halves(u, src):
+        if GATHERED[u] == 2:
+            return H[u].at[src, 0], H[u].at[src, 1]
+        if WIDTH[u] == 256:
+            return H[u].at[src, :, :, pl.ds(0, 128)], H[u].at[src, :, :, pl.ds(128, 128)]
+        return H[u].at[src], None
+
+    def relay(u):
+        for side, sem in ((0, ag_low), (1, ag_high)):
+            src = lax.rem(y + (6, 2)[side], 8)
+            got, part = H[u].at[src], halves(u, src)[side]
+            await_recv(got, sem.at[u])
+            if part is not None:
+                to = along_y(lax.rem(y + (2, 6)[side], 8))
+                remote(part, part, ag_send.at[u], ag_recv.at[u], to).start()
+            to = along_y(lax.rem(y + (1, 7)[side], 8))
+            remote(got, got, ag_send.at[u], ag_recv.at[u], to).start()
 
     def mix(f):
         u = GU[f]
-        await_recv(H[u].at[pl.ds(0, 7)], ag_recv.at[u])
+        await_recv(H[u].at[pl.ds(0, 5)], ag_recv.at[u])
         hid = H[u][:, 0].reshape(128, WIDTH[u])
         acc_m[...] += jnp.dot(hid, weight(DN[f], 0), preferred_element_type=F32)
 
     def grads(f):
         u = DN[f]
-        await_recv(H[u].at[pl.ds(0, 7)], ag_recv.at[u])
+        await_recv(H[u].at[pl.ds(0, 5)], ag_recv.at[u])
         gg, ug = (H[u][:, w].reshape(128, WIDTH[u]) for w in range(2))
         acc_g[...] += jnp.dot(gg, weight(GU[f], 0), preferred_element_type=F32) + jnp.dot(
             ug, weight(GU[f], 1), preferred_element_type=F32
@@ -215,33 +239,15 @@
 
     accs, outs = (acc_m, acc_g), (mixed_out, grad_out)
 
-    def near_start(a):
+    def scatter(a):
         for e in range(16):
             for v in range(2):
-                O[a, e % 4, e // 4, v] = accs[a][
-                    e * 8 : e * 8 + 8, v * 512 : v * 512 + 512
-                ].astype(BF16)
-        for k in (3, 2, 1):
-            to = lax.rem(zl + k, 4)
-            remote(
-                O.at[a, to], Q.at[a, k - 1], q_send.at[a], q_recv.at[a], (zh * 4 + to, t, s)
-            ).start()
-
-    def far_start(a):
-        await_recv(Q.at[a], q_recv.at[a])
-        for e in range(4):
+                O[a, e, v] = accs[a][e * 8 : e * 8 + 8, v * 512 : v * 512 + 512].astype(BF16)
+        for k in FAR_FIRST:
+            to = lax.rem(d + k, 16)
             for v in range(2):
-                part = accs[a][
-                    pl.ds(pl.multiple_of(e * 32 + zl * 8, 8), 8), v * 512 : v * 512 + 512
-                ]
-                for k in range(3):
-                    part = part + Q[a, k, e, v].astype(F32)
-                O2[a, e, v] = part.astype(BF16)
-        for k in (2, 1, 3, 0):
-            to = lax.rem(zh + k, 4)
-            for v in range(2):
-                src, dst = O2.at[a, to, v], Z.at[a, h * 4 + zh]
-                dev = (to * 4 + zl, 2 * yl + v, x * 2 + c)
+                src, dst = O.at[a, to, v], Z.at[a, h * 16 + d]
+                dev = (to, 2 * yl + v, x * 2 + c)
                 if k:
                     remote(src, dst, z_send.at[a], z_recv.at[a], dev).start()
                 else:
@@ -258,9 +264,9 @@
     def finish(a):
         await_recv(Z.at[a], z_recv.at[a])
         for b in range(2):
-            total = Z[a, b * 4].astype(F32)
-            for k in range(1, 4):
-                total = total + Z[a, b * 4 + k].astype(F32)
+            total = Z[a, b * 16].astype(F32)
+            for k in range(1, 16):
+                total = total + Z[a, b * 16 + k].astype(F32)
             for e in range(4):
                 to = (e * 2 + b) * 128
                 outs[a][:, to : to + 128] = total[:, e * 128 : e * 128 + 128].astype(BF16)
@@ -272,21 +278,28 @@
         if i < M:
             take_opposite(i)
             if i == 0:
-                await_recv(X, x_recv)
+                await_recv(X.at[0], x_recv.at[0])
+            if i == DN[0]:
+                await_recv(X.at[1], x_recv.at[1])
             partial_sums(i)
+            if i < len(REACH):
+                pl.semaphore_wait(ready.at[i], 2)
+                if i + 1 < len(REACH):
+                    tell(i + 1)
         if i >= 2:
             activate(i - 2)
+        if i >= 3:
+            relay(i - 3)
         if i < M and UNITS[i][0] == "dn":
             mix(UNITS[i][1])
             if i == M - 1:
-                near_start(0)
+                scatter(0)
         if i >= 4 and UNITS[i - 4][0] == "dn":
             grads(UNITS[i - 4][1])
-    far_start(0)
+    relay(M - 1)
     grads(UNITS[M - 2][1])
     grads(UNITS[M - 1][1])
-    near_start(1)
-    far_start(1)
+    scatter(1)
     finish(0)
     finish(1)
 
@@ -294,14 +307,11 @@
         await_send(W[u].at[:, pl.ds(0, 7)], w_send.at[u])
         await_send(R[u], rs_send.at[u])
         await_send(H[u].at[pl.ds(0, 7)], ag_send.at[u])
-    for a in range(2):
-        await_send(Q.at[a], q_send.at[a])
-
     @pl.when(c == h)
     def _():
         await_send(X.at[:, :, pl.ds(0, 512)], x_send)
         for a in range(2):
-            await_send(Z.at[a, pl.ds(0, 7)], z_send.at[a])
+            await_send(Z.at[a, pl.ds(0, 31)], z_send.at[a])
 
     @pl.when(c != h)
     def _():
@@ -324,15 +334,13 @@
     scratch += [
         vmem((128, 1024), F32),
         vmem((128, 1024), F32),
-        vmem((2, 4, 4, 2, 8, 512), BF16),
-        vmem((2, 3, 4, 2, 8, 512), BF16),
-        vmem((2, 4, 2, 8, 512), BF16),
-        vmem((2, 8, 8, 512), BF16),
+        vmem((2, 16, 2, 8, 512), BF16),
+        vmem((2, 32, 8, 512), BF16),
     ]
-    scratch += [dma, dma((M,)), dma, dma]
+    scratch += [dma, dma((M,)), dma, dma((2,))]
     scratch += [dma((M,))] * 5
-    scratch += [dma((M,))] * 4
-    scratch += [dma((2,))] * 4
+    scratch += [dma((M,))] * 6
+    scratch += [dma((2,))] * 2 + [pltpu.SemaphoreType.REGULAR((len(REACH),))]
     return pl.pallas_call(
         kernel,
         out_shape=[jax.ShapeDtypeStruct((8, 1024), BF16)] * 2,

time: 100 us -> 94.6 us (0.946)
  Pallas kernels: 97.4 us -> 91.9 us
    pallas_call x1, Pallas kernels: 97.4 us -> 91.9 us  [body(): pl.pallas_call(kernel, out_shape=[jax.ShapeDtypeStruct((8, 1024), BF16)]...]
where the time goes in v3:
time: 94.6 us; the launch traced here: 94.4 us
  Pallas kernels  91.9 us (97%)
  local copies, waits for them, and re-layouts  1.94 us (2%)
    pallas_call x1, Pallas kernels, body(): pl.pallas_call(kernel, out_shape=[jax.ShapeDtypeStruct((8, 1024), BF16)]...  91.9 us
    unnamed x4, local copies, waits for them, and re-layouts  1.94 us

profile of v3, /device:TPU:1, one launch (start us, length us, event | category | flops | bytes accessed | tf_op | source)
XLA Modules:
  0.0 94.4 jit_solution(11159842788197995408)
XLA Ops:
  0.6 91.9 %ffn.1 = (bf16[8,1024]{1,0:T(8,128)(2,1)}, bf16[8,1024]{1,0:T(8,128)(2,1)}) custom-call(bf16[128,1024]{1,0:T(8,128)(2,1)} %refs_0_.1, bf16[128,1024]{1,0:T(8,128)(2,1)} %refs_1_.1, bf16[960,128]{1,0:T(8,128)(2,1)} %bitcast.3, bf16[960,128]{1,0:T(8,128)(2,1)} %bitcast.4, bf16[960,128]{1,0:T(8,128)(2,1)} %bitcast.5), custom_call_target="tpu_custom_call" | custom-call | tf_op jit(solution)/shard_map/ffn/pallas_call | solution.py:344
  92.5 0.0 copy-start
  92.5 1.3 %copy.9 = bf16[8,1024]{1,0:T(8,128)(2,1)} copy(bf16[8,1024]{1,0:T(8,128)(2,1)} %get-tuple-element.4) | data formatting | bytes 32768
  93.8 0.0 copy-done
  93.8 0.6 copy.10
Async XLA Ops:
  92.5 1.3 %copy-start = (bf16[8,1024]{1,0:T(8,128)(2,1)S(1)}, bf16[8,1024]{1,0:T(8,128)(2,1)}, u32[]{:S(2)}) copy-start(bf16[8,1024]{1,0:T(8,128)(2,1)} %get-tuple-element.5) | copy-start | bytes 49156

commit v4 on v3

--- a/solution.py
+++ b/solution.py
@@ -31,7 +31,7 @@
         return out
 
     tok, cot, gate_w, up_w, down_w = take(5)
-    mixed_out, grad_out = take(2)
+    (out,) = take(1)
     T, X = take(2)
     W, Pt, Pf, R, H = take(M), take(M), take(M), take(M), take(M)
     G = take(N)
@@ -237,7 +237,7 @@
             ug, weight(GU[f], 1), preferred_element_type=F32
         )
 
-    accs, outs = (acc_m, acc_g), (mixed_out, grad_out)
+    accs = (acc_m, acc_g)
 
     def scatter(a):
         for e in range(16):
@@ -269,7 +269,7 @@
                 total = total + Z[a, b * 16 + k].astype(F32)
             for e in range(4):
                 to = (e * 2 + b) * 128
-                outs[a][:, to : to + 128] = total[:, e * 128 : e * 128 + 128].astype(BF16)
+                out[a, :, to : to + 128] = total[:, e * 128 : e * 128 + 128].astype(BF16)
 
     take_neighbours(0)
     for i in range(M + 2):
@@ -341,15 +341,16 @@
     scratch += [dma((M,))] * 5
     scratch += [dma((M,))] * 6
     scratch += [dma((2,))] * 2 + [pltpu.SemaphoreType.REGULAR((len(REACH),))]
-    return pl.pallas_call(
+    both = pl.pallas_call(
         kernel,
-        out_shape=[jax.ShapeDtypeStruct((8, 1024), BF16)] * 2,
+        out_shape=jax.ShapeDtypeStruct((2, 8, 1024), BF16),
         in_specs=[pl.BlockSpec(memory_space=pl.ANY)] * 5,
-        out_specs=[pl.BlockSpec(memory_space=pltpu.VMEM)] * 2,
+        out_specs=pl.BlockSpec(memory_space=pltpu.VMEM),
         scratch_shapes=scratch,
         compiler_params=pltpu.CompilerParams(collective_id=0, has_side_effects=True),
         name="ffn",
     )(tokens, cotangent, gate_weight.T, up_weight.T, down_weight.T)
+    return both[0], both[1]
 
 
 def solution(mesh):

time: 94.6 us -> 93.8 us (level)
    unnamed x4 -> x0, local copies, waits for them, and re-layouts: 1.94 us -> none
    squeeze x0 -> x1, local copies, waits for them, and re-layouts: none -> 1.35 us  [body(): return (both[0], both[1])]
where the time goes in v4:
time: 93.8 us; the launch traced here: 93.6 us
  Pallas kernels  91.6 us (98%)
  local copies, waits for them, and re-layouts  1.35 us (1%)
    pallas_call x1, Pallas kernels, body(): pl.pallas_call(kernel, out_shape=jax.ShapeDtypeStruct((2, 8, 1024), BF16)...  91.6 us

profile of v4, /device:TPU:1, one launch (start us, length us, event | category | flops | bytes accessed | tf_op | source)
XLA Modules:
  0.0 93.6 jit_solution(6420532095391756517)
XLA Ops:
  0.6 91.6 %ffn.1 = bf16[2,8,1024]{2,1,0:T(8,128)(2,1)} custom-call(bf16[128,1024]{1,0:T(8,128)(2,1)} %refs_0_.1, bf16[128,1024]{1,0:T(8,128)(2,1)} %refs_1_.1, bf16[960,128]{1,0:T(8,128)(2,1)} %bitcast.7, bf16[960,128]{1,0:T(8,128)(2,1)} %bitcast.8, bf16[960,128]{1,0:T(8,128)(2,1)} %bitcast.9), custom_call_target="tpu_custom_call" | custom-call | tf_op jit(solution)/shard_map/ffn/pallas_call | solution.py:344
  92.2 1.3 %slice_bitcast_fusion = (bf16[8,1024]{1,0:T(8,128)(2,1)}, bf16[8,1024]{1,0:T(8,128)(2,1)}) fusion(bf16[2,8,1024]{2,1,0:T(8,128)(2,1)} %ffn.1), kind=kLoop, calls=%fused_computation | loop fusion | bytes 65536 | tf_op jit(solution)/shard_map/squeeze | solution.py:353
